TPU v7x, 256 devices: a 8x8x2 block of a 8x8x16 slice. The times are simulated.
256 devices in a mesh: groups: 2 (over z), psg: 128 (over x, y, core).
Axes of the slice: x: 8, y: 8, z: 2, core: 2. Of those that a mesh axis runs over, the one named last changes fastest.
The devices are a block of a 8x8x16 slice.
Arguments:
- queries: bfloat16 [512, 32, 128], P(('groups', 'psg')), parts along dimension 0, may hold values from -0.29882812 to 0.29882812
- candidates: int32 [512, 512], P(('groups', 'psg')), parts along dimension 0, may hold values from 0 to 1279
- centroids: bfloat16 [65536, 128], P('psg'), may hold values from -6 to 6
- bucket_weights: float32 [4, 128], replicated, may hold values from -1 to 1
- centroid_shard: int32 [262144, 1], P('psg'), may hold values from 0 to 127; in each aligned block of 2048 rows (0 to 2047, 2048 to 4095, ...) at most 32 rows name the same one
- centroid_row: int32 [262144], P('psg'), may hold values from 0 to 511
- residual_codes: int32 [262144, 128], P('psg'), may hold values from 0 to 3
- tile_count: int32 [1280], replicated, may hold values from 1 to 3, 2048 in all
- last_fill: int32 [1280], replicated, may hold values from 1 to 128
Outputs:
- scores: float32 [512, 512], P(('groups', 'psg')), parts along dimension 0
There are 2 independent parts, one for each index of `groups`. A program takes and returns all parts, laid end to end along the dimension named above; an argument that names none is the same for every part. Nothing has to cross between parts.
Inputs may be any that keep to these rules, and one draw needn't show every extreme that they name: `tile_count`: tiles are numbered along psg, device k holding tiles k * 16 onward; the counts sum to 2048, so a passage may continue on the next device. `centroid_shard`: among the 2048 token slots of one device, at most 32 name the same device; on some device some value is named exactly 32 times.
All inputs are finite; a program needn't handle non-finite values.
Results may differ from a plain program's by a relative error of at most 0.0003.
Values may be sent and summed in bfloat16 or wider, within the bound.
A program may use at most 64 MiB of HBM per device.

v0:
```python
import functools

import jax
import jax.numpy as jnp
from jax import lax
from jax.experimental import pallas as pl
from jax.experimental.pallas import tpu as pltpu
from jax.sharding import PartitionSpec as P

MESH = pl.DeviceIdType.MESH
TILE = 128
LANES = 128
NX, NY, NC = 8, 8, 2
CAP = 32
EPS = 1e-06
F32, BF16, I32 = jnp.float32, jnp.bfloat16, jnp.int32


def dot(a, b, ca=1, cb=0):
    return lax.dot_general(a, b, (((ca,), (cb,)), ((), ())), preferred_element_type=F32)


def kernel(
    owner_ref,
    row_ref,
    cent_hbm,
    code_hbm,
    bw_ref,
    count_ref,
    last_ref,
    query_ref,
    cand_ref,
    out_ref,
    cent,
    code,
    req,
    asked,
    onehot,
    sent,
    fetched,
    low,
    high,
    res,
    acc,
    emb,
    qb,
    tm,
    head_out,
    head_in,
    wide,
    got,
    starts,
    fills,
    join1,
    join2,
    load_sem,
    req_send,
    req_recv,
    row_send,
    row_recv,
    qx_send,
    qx_recv,
    qup_send,
    qup_recv,
    qdn_send,
    qdn_recv,
    qc_send,
    qc_recv,
    head_send,
    head_recv,
    score_send,
    score_recv,
):
    n = NX * NY * NC
    tiles = owner_ref.shape[0]
    npass = count_ref.shape[0]
    me = lax.axis_index("psg")
    x = me // (NY * NC)
    y = lax.rem(me // NC, NY)
    c = lax.rem(me, NC)
    other = 1 - c

    def index(px, py, pc):
        return (px * NY + py) * NC + pc

    def ahead(g, a, k):
        px, py = lax.rem(x + a, NX), lax.rem(y + a + g, NY)
        return px, py, index(px, py, c if k == 0 else other)

    def behind(g, a, k):
        px, py = lax.rem(x + NX - a, NX), lax.rem(y + 2 * NY - a - g, NY)
        return index(px, py, c if k == 0 else other)

    def relative(device):
        dx = (x - device // (NY * NC)) & (NX - 1)
        dy = (y - (device // NC) % NY) & (NY - 1)
        dc = (c - device) & (NC - 1)
        return ((dy - dx) & (NY - 1)) * (NX * NC) + dx * NC + dc

    pairs = [(a, k) for a in range(NX) for k in range(NC)]
    group = NX * NC
    gslots = group * CAP

    barrier = pltpu.get_barrier_semaphore()
    for g in range(NY):
        for a, k in pairs:
            if (g, a, k) != (0, 0, 0):
                pl.semaphore_signal(
                    barrier, inc=1, device_id={"psg": ahead(g, a, k)[2]}, device_id_type=MESH
                )
    cent_copy = pltpu.make_async_copy(cent_hbm, cent, load_sem.at[0])
    cent_copy.start()
    code_copy = pltpu.make_async_copy(code_hbm, code, load_sem.at[1])
    code_copy.start()

    sub = lax.broadcasted_iota(I32, (LANES, LANES), 0)
    lane = lax.broadcasted_iota(I32, (LANES, LANES), 1)
    upper = (sub <= lane).astype(BF16)
    ones = jnp.ones((LANES, LANES), BF16)
    rel = relative(owner_ref[...])
    crow = row_ref[...]
    carry = jnp.zeros((LANES, LANES), F32)
    low_sum = jnp.zeros((LANES, LANES), F32)
    high_sum = jnp.zeros((LANES, LANES), F32)
    slots = []
    for t in range(tiles):
        member = sub == rel[t : t + 1, :]
        flags = member.astype(BF16)
        running = dot(flags, upper) + carry
        carry = carry + dot(flags, ones)
        rank = jnp.sum(jnp.where(member, running, 0.0), axis=0, keepdims=True).astype(I32) - 1
        slots.append(rel[t : t + 1, :] * CAP + rank)
        place = sub == rank
        tok = crow[t : t + 1, :]
        low_sum = low_sum + dot(
            flags, jnp.where(place, (tok & 255).astype(F32), 0.0).astype(BF16), 1, 1
        )
        high_sum = high_sum + dot(
            flags, jnp.where(place, (tok >> 8).astype(F32), 0.0).astype(BF16), 1, 1
        )
    req[...] = (low_sum + 256.0 * high_sum).astype(I32)

    pl.semaphore_wait(barrier, n - 1)
    asked[0:1, :] = req[0:1, :]
    for g in range(NY):
        for a, k in pairs:
            if (g, a, k) != (0, 0, 0):
                j = g * group + a * NC + k
                pltpu.make_async_remote_copy(
                    src_ref=req.at[pl.ds(j, 1)],
                    dst_ref=asked.at[pl.ds(j, 1)],
                    send_sem=req_send,
                    recv_sem=req_recv.at[g],
                    device_id={"psg": behind(g, a, k)},
                    device_id_type=MESH,
                ).start()

    nq = query_ref.shape[0]
    for a in range(1, NX):
        px = lax.rem(x + a, NX)
        pltpu.make_async_remote_copy(
            src_ref=query_ref,
            dst_ref=qb.at[y, c, pl.ds(pl.multiple_of(x * nq, nq), nq)],
            send_sem=qx_send,
            recv_sem=qx_recv,
            device_id={"psg": index(px, y, c)},
            device_id_type=MESH,
        ).start()
    qb[y, c, pl.ds(pl.multiple_of(x * nq, nq), nq), :] = query_ref[...]

    slot = jnp.concatenate(slots, axis=0)
    pad = jnp.zeros((LANES - tiles, LANES), F32)
    low_t = jnp.concatenate([(slot & 255).astype(F32), pad], axis=0).T
    high_t = jnp.concatenate([(slot >> 8).astype(F32), pad], axis=0).T
    wide_lane = lax.broadcasted_iota(I32, (LANES, 256), 1).astype(F32)
    for t in range(tiles):
        at = pl.ds(t * TILE, TILE)
        low[at, :] = (low_t[:, t : t + 1] == wide_lane).astype(BF16)
        high[at, :] = jnp.broadcast_to(high_t[:, t : t + 1], (TILE, LANES))

    counts = count_ref[...].astype(F32)
    sums = dot(counts.astype(BF16), upper)
    before = jnp.zeros((1, 1), F32)
    rows = []
    for r in range(npass):
        rows.append(sums[r : r + 1, :] + before)
        before = before + sums[r : r + 1, LANES - 1 : LANES]
    ends = jnp.concatenate(rows, axis=0)
    starts[...] = (ends - counts).astype(I32)
    final = ends.astype(I32) - 1
    last = last_ref[...].astype(F32)
    fill_rows, end_rows = [], []
    for t in range(tiles + 1):
        hit = final == me * tiles + t
        fill_rows.append(jnp.sum(jnp.where(hit, last, 0.0), axis=0, keepdims=True))
        end_rows.append(jnp.sum(jnp.where(hit, 1.0, 0.0), axis=0, keepdims=True))
    fill = jnp.sum(jnp.concatenate(fill_rows, axis=0), axis=1, keepdims=True)
    ending = jnp.sum(jnp.concatenate(end_rows, axis=0), axis=1, keepdims=True)
    fills[...] = jnp.broadcast_to(jnp.where(ending > 0, fill, float(TILE))[:tiles], (tiles, LANES))
    goes = ending == 0
    join1[...] = jnp.broadcast_to(goes[:tiles].astype(F32), (tiles, LANES))
    join2[...] = jnp.broadcast_to(
        goes[:tiles].astype(F32) * goes[1 : tiles + 1].astype(F32), (tiles, LANES)
    )

    up = index(x, lax.rem(y + 1, NY), c)
    down = index(x, lax.rem(y + NY - 1, NY), c)
    across = index(x, y, other)
    n_up, n_down = NY // 2, NY - 1 - NY // 2

    def pass_on(block, where, send, recv):
        pltpu.make_async_remote_copy(
            src_ref=qb.at[block, c],
            dst_ref=qb.at[block, c],
            send_sem=send,
            recv_sem=recv,
            device_id={"psg": where},
            device_id_type=MESH,
        ).start()

    def arrived(ref, sem):
        pltpu.make_async_copy(ref, ref, sem).wait()

    arrived(qb.at[y, c, pl.ds(0, (NX - 1) * nq)], qx_recv)
    pass_on(y, up, qup_send, qup_recv.at[0])
    pass_on(y, down, qdn_send, qdn_recv.at[0])
    pass_on(y, across, qc_send, qc_recv)

    cent_copy.wait()
    half_lane = lax.broadcasted_iota(I32, (CAP, cent.shape[0]), 1).astype(F32)

    def ring(s):
        block = lax.rem(y + NY - s, NY)
        arrived(qb.at[block, c], qup_recv.at[s - 1])
        if s < n_up:
            pass_on(block, up, qup_send, qup_recv.at[s])
        pass_on(block, across, qc_send, qc_recv)
        if s <= n_down:
            block = lax.rem(y + s, NY)
            arrived(qb.at[block, c], qdn_recv.at[s - 1])
            if s < n_down:
                pass_on(block, down, qdn_send, qdn_recv.at[s])
            pass_on(block, across, qc_send, qc_recv)

    for g in range(NY):
        count = group - 1 if g == 0 else group
        arrived(asked.at[pl.ds(0, count)], req_recv.at[g])
        wanted = asked[pl.ds(g * group, group), :].astype(F32).T
        for j in range(group):
            onehot[pl.ds(j * CAP, CAP), :] = (wanted[:CAP, j : j + 1] == half_lane).astype(BF16)
        found = dot(onehot[...], cent[...]).astype(BF16)
        sent[pl.ds(g * gslots, gslots), :] = found
        if g == 0:
            fetched[pl.ds(0, CAP), :] = found[:CAP]
        for a, k in pairs:
            if (g, a, k) != (0, 0, 0):
                at = pl.ds((g * group + a * NC + k) * CAP, CAP)
                pltpu.make_async_remote_copy(
                    src_ref=sent.at[at],
                    dst_ref=fetched.at[at],
                    send_sem=row_send,
                    recv_sem=row_recv.at[g],
                    device_id={"psg": ahead(g, a, k)[2]},
                    device_id_type=MESH,
                ).start()
        if g % 2 == 0:
            ring(g // 2 + 1)

    code_copy.wait()

    @pl.loop(0, tiles)
    def _(t):
        at = pl.ds(pl.multiple_of(t * TILE, TILE), TILE)
        v = code[at, :]
        first = jnp.where(v == 0, bw_ref[0:1, :], bw_ref[1:2, :])
        second = jnp.where(v == 2, bw_ref[2:3, :], bw_ref[3:4, :])
        res[at, :] = jnp.where(v < 2, first, second)

    span = 4 * TILE
    for g in range(NY):
        count = (group - 1 if g == 0 else group) * CAP
        arrived(fetched.at[pl.ds(0, count)], row_recv.at[g])
        base = g * gslots
        both = jnp.concatenate(
            [fetched[pl.ds(base, 256), :], fetched[pl.ds(base + 256, 256), :]], axis=1
        )

        @pl.loop(0, tiles * TILE // span)
        def _(i):
            at = pl.ds(pl.multiple_of(i * span, span), span)
            picked = dot(low[at, :], both)
            which = high[at, :]
            keep = 0.0 if g == 0 else acc[at, :]
            keep = jnp.where(which == float(2 * g + 1), picked[:, LANES:], keep)
            acc[at, :] = jnp.where(which == float(2 * g), picked[:, :LANES], keep)

    @pl.loop(0, tiles)
    def _(t):
        at = pl.ds(pl.multiple_of(t * TILE, TILE), TILE)
        summed = acc[at, :] + res[at, :]
        scale = lax.rsqrt(jnp.sum(summed * summed, axis=1, keepdims=True) + EPS)
        unit = summed * scale
        unit = jnp.where(sub.astype(F32) < fills[pl.ds(t, 1), :], unit, unit[0:1, :])
        emb[at, :] = unit.astype(BF16)

    arrived(qb.at[pl.ds(0, NY), 0], qc_recv)

    span = tiles // 2
    chunk = 256
    per = qb.shape[2] // chunk

    def maxima(half):
        @pl.loop(0, NY * NC * per)
        def _(i):
            part = qb[
                i // (NC * per),
                lax.rem(i // per, NC),
                pl.ds(pl.multiple_of(lax.rem(i, per) * chunk, chunk), chunk),
                :,
            ]
            at = pl.ds(pl.multiple_of(i * chunk, chunk), chunk)
            s = dot(emb[pl.ds(half * span * TILE, span * TILE), :], part, 1, 1)
            top = jnp.max(s.reshape(span, TILE, chunk), axis=1)
            tm[pl.ds(half * span, span), at] = top
            if half == 0:
                head_out[:, at] = top[0:2, :]

    maxima(0)
    pltpu.make_async_remote_copy(
        src_ref=head_out,
        dst_ref=head_in,
        send_sem=head_send,
        recv_sem=head_recv,
        device_id={"psg": lax.rem(me + n - 1, n)},
        device_id_type=MESH,
    ).start()
    maxima(1)
    arrived(head_in, head_recv)
    tm[tiles : tiles + 2, :] = head_in[...]

    width = NX * LANES
    first_join, second_join = join1[...] > 0, join2[...] > 0
    for b in range(NY):
        stack = []
        for i in range(NX):
            at = pl.ds(b * width + i * LANES, LANES)
            one = tm[0:tiles, at]
            one = jnp.maximum(one, jnp.where(first_join, tm[1 : tiles + 1, at], one))
            one = jnp.maximum(one, jnp.where(second_join, tm[2 : tiles + 2, at], one))
            stack.append(one)
        turned = jnp.concatenate(stack, axis=0).T
        total = jnp.sum(turned.reshape(4, 32, LANES), axis=1)
        wide[2 * b] = total[0:2]
        wide[2 * b + 1] = total[2:4]

    for g in range(NY):
        for a, k in pairs:
            j = g * group + a * NC + k
            if j == 0:
                got[0] = wide[y * 2 + lax.rem(x, 2)]
                continue
            px, py, peer = ahead(g, a, k)
            pltpu.make_async_remote_copy(
                src_ref=wide.at[py * 2 + lax.rem(px, 2)],
                dst_ref=got.at[j],
                send_sem=score_send,
                recv_sem=score_recv,
                device_id={"psg": peer},
                device_id_type=MESH,
            ).start()

    cand = cand_ref[...]
    tile = jnp.zeros(cand.shape, I32)
    for r in range(npass):
        table = jnp.broadcast_to(starts[r : r + 1, :], cand.shape)
        value = jnp.take_along_axis(table, cand & (LANES - 1), axis=1)
        tile = jnp.where(cand >> 7 == r, value, tile)
    source, slot_of = relative(tile // tiles), tile % tiles
    upper_half = lax.broadcasted_iota(I32, cand.shape, 0) < cand.shape[0] // 2
    turn = lax.rem(LANES - (c * (NX // 2) + x // 2) * tiles, LANES)

    arrived(got.at[pl.ds(0, n - 1)], score_recv)
    tables = [pltpu.roll(got[:, i, :], turn, 1).T for i in range(2)]
    score = jnp.zeros(cand.shape, F32)
    for s in range(tiles):
        table = jnp.where(upper_half, tables[0][s : s + 1, :], tables[1][s : s + 1, :])
        value = jnp.take_along_axis(table, source, axis=1)
        score = jnp.where(slot_of == s, value, score)
    out_ref[...] = score

    arrived(req.at[pl.ds(0, n - 1)], req_send)
    arrived(sent.at[pl.ds(0, (n - 1) * CAP)], row_send)
    arrived(qb.at[0, 0, pl.ds(0, (NX - 1) * nq)], qx_send)
    arrived(qb.at[pl.ds(0, n_up), 0], qup_send)
    arrived(qb.at[pl.ds(0, n_down), 0], qdn_send)
    arrived(qb.at[pl.ds(0, NY), 0], qc_send)
    arrived(head_out, head_send)
    arrived(got.at[pl.ds(0, n - 1)], score_send)


def per_device(
    queries,
    candidates,
    centroids,
    bucket_weights,
    centroid_shard,
    centroid_row,
    residual_codes,
    tile_count,
    last_fill,
):
    n = NX * NY * NC
    tok, dim = residual_codes.shape
    tiles = tok // TILE
    nq = queries.shape[0] * queries.shape[1]
    ncand = candidates.size // LANES
    npass = tile_count.shape[0] // LANES
    dma = pltpu.SemaphoreType.DMA
    vmem = pl.BlockSpec(memory_space=pltpu.VMEM)
    anywhere = pl.BlockSpec(memory_space=pl.ANY)
    score = pl.pallas_call(
        kernel,
        out_shape=jax.ShapeDtypeStruct((ncand, LANES), F32),
        in_specs=[vmem, vmem, anywhere, anywhere, vmem, vmem, vmem, vmem, vmem],
        out_specs=vmem,
        scratch_shapes=[
            pltpu.VMEM(centroids.shape, BF16),
            pltpu.VMEM(residual_codes.shape, I32),
            pltpu.VMEM((n, LANES), I32),
            pltpu.VMEM((n, LANES), I32),
            pltpu.VMEM((NX * NC * CAP, centroids.shape[0]), BF16),
            pltpu.VMEM((n * CAP, dim), BF16),
            pltpu.VMEM((n * CAP, dim), BF16),
            pltpu.VMEM((tok, 256), BF16),
            pltpu.VMEM((tok, LANES), F32),
            pltpu.VMEM((tok, dim), F32),
            pltpu.VMEM((tok, dim), F32),
            pltpu.VMEM((tok, dim), BF16),
            pltpu.VMEM((NY, NC, NX * nq, dim), BF16),
            pltpu.VMEM((tiles + 8, n * nq), F32),
            pltpu.VMEM((2, n * nq), F32),
            pltpu.VMEM((2, n * nq), F32),
            pltpu.VMEM((2 * NY, 2, LANES), F32),
            pltpu.VMEM((n, 2, LANES), F32),
            pltpu.VMEM((npass, LANES), I32),
            pltpu.VMEM((tiles, LANES), F32),
            pltpu.VMEM((tiles, LANES), F32),
            pltpu.VMEM((tiles, LANES), F32),
            dma((2,)),
            dma,
            dma((NY,)),
            dma,
            dma((NY,)),
            dma,
            dma,
            dma,
            dma((NY // 2,)),
            dma,
            dma((NY // 2,)),
            dma,
            dma,
            dma,
            dma,
            dma,
            dma,
        ],
        compiler_params=pltpu.CompilerParams(collective_id=0, has_side_effects=True),
    )(
        centroid_shard.reshape(tiles, TILE),
        centroid_row.reshape(tiles, TILE),
        centroids,
        residual_codes,
        bucket_weights,
        tile_count.reshape(npass, LANES),
        last_fill.reshape(npass, LANES),
        queries.reshape(nq, dim),
        candidates.reshape(ncand, LANES),
    )
    return score.reshape(candidates.shape)


def solution(mesh):
    both = ("groups", "psg")
    return jax.shard_map(
        per_device,
        mesh=mesh,
        in_specs=(
            P(both, None, None),
            P(both, None),
            P("psg", None),
            P(),
            P("psg", None),
            P("psg"),
            P("psg", None),
            P(),
            P(),
        ),
        out_specs=P(both, None),
        check_vma=False,
    )
```

profile of v0, /device:TPU:513, one launch (start us, length us, event | category | flops | bytes accessed | tf_op | source)
XLA Modules:
  0.0 114.8 jit_solution(14435119328867511110)
XLA Ops:
  0.0 0.0 copy-start
  0.0 0.7 copy-done
  0.7 0.6 reshape.26.cand_ref
  1.3 112.2 %shard_map.91 = f32[8,128]{1,0:T(8,128)} custom-call(s32[16,128]{1,0:T(8,128)} %bitcast.6, s32[16,128]{1,0:T(8,128)} %bitcast.7, bf16[512,128]{1,0:T(8,128)(2,1)} %cent_hbm.1, s32[2048,128]{1,0:T(8,128)} %code_hbm.1, f32[4,128]{1,0:T(4,128)} %bw_ref.1, s32[10,128]{1,0:T(8,128)} %bitcast.8, s32[10,128]{1,0:T(8,128)} %bitcast.9, bf16[64,128]{1,0:T(8,128)(2,1)} %bitcast.5, ...), custom_call_target="tpu_custom_call" | custom-call | tf_op jit(solution)/shard_map/pallas_call | solution.py:421
  113.5 1.3 %reshape.27 = f32[2,512]{1,0:T(2,128)} reshape(f32[8,128]{1,0:T(8,128)} %shard_map.91) | data formatting | bytes 8192 | tf_op jit(solution)/shard_map/reshape | solution.py:479
Async XLA Ops:
  0.0 0.7 copy-start
where the time goes:
time: 115 us
  Pallas kernels  112 us (97%)
  local copies, waits for them, and re-layouts  2.56 us (2%)
    pallas_call x1, Pallas kernels, per_device(): pl.pallas_call(kernel, out_shape=jax.ShapeDtypeStruct((ncand, LANES), F32...  112 us

commit v1 on v0

--- a/solution.py
+++ b/solution.py
@@ -34,6 +34,7 @@
     cent,
     code,
     req,
+    mid_req,
     asked,
     onehot,
     sent,
@@ -48,14 +49,17 @@
     head_out,
     head_in,
     wide,
+    mid,
     got,
     starts,
     fills,
     join1,
     join2,
     load_sem,
-    req_send,
-    req_recv,
+    rx_send,
+    rx_recv,
+    ry_send,
+    ry_recv,
     row_send,
     row_recv,
     qx_send,
@@ -68,8 +72,10 @@
     qc_recv,
     head_send,
     head_recv,
-    score_send,
-    score_recv,
+    s1_send,
+    s1_recv,
+    s2_send,
+    s2_recv,
 ):
     n = NX * NY * NC
     tiles = owner_ref.shape[0]
@@ -87,15 +93,29 @@
         px, py = lax.rem(x + a, NX), lax.rem(y + a + g, NY)
         return px, py, index(px, py, c if k == 0 else other)
 
-    def behind(g, a, k):
-        px, py = lax.rem(x + NX - a, NX), lax.rem(y + 2 * NY - a - g, NY)
-        return index(px, py, c if k == 0 else other)
-
-    def relative(device):
+    def shift(device):
         dx = (x - device // (NY * NC)) & (NX - 1)
         dy = (y - (device // NC) % NY) & (NY - 1)
         dc = (c - device) & (NC - 1)
-        return ((dy - dx) & (NY - 1)) * (NX * NC) + dx * NC + dc
+        return dx, dy, dc
+
+    def push(src, dst, where, send, recv):
+        pltpu.make_async_remote_copy(
+            src_ref=src,
+            dst_ref=dst,
+            send_sem=send,
+            recv_sem=recv,
+            device_id={"psg": where},
+            device_id_type=MESH,
+        ).start()
+
+    def arrived(ref, sem):
+        pltpu.make_async_copy(ref, ref, sem).wait()
+
+    def at_uv(u, v):
+        return (1 - c) * index(v, u, 0) + c * index(u, v, 1)
+
+    u, v = y + c * (x - y), x + c * (y - x)
 
     pairs = [(a, k) for a in range(NX) for k in range(NC)]
     group = NX * NC
@@ -117,7 +137,9 @@
     lane = lax.broadcasted_iota(I32, (LANES, LANES), 1)
     upper = (sub <= lane).astype(BF16)
     ones = jnp.ones((LANES, LANES), BF16)
-    rel = relative(owner_ref[...])
+    dx, dy, dc = shift(owner_ref[...])
+    rel = (dx * NY + dy) * NC + dc
+    turn_of = ((dy - dx) & (NY - 1)) * (NX * NC) + dx * NC + dc
     crow = row_ref[...]
     carry = jnp.zeros((LANES, LANES), F32)
     low_sum = jnp.zeros((LANES, LANES), F32)
@@ -129,7 +151,7 @@
         running = dot(flags, upper) + carry
         carry = carry + dot(flags, ones)
         rank = jnp.sum(jnp.where(member, running, 0.0), axis=0, keepdims=True).astype(I32) - 1
-        slots.append(rel[t : t + 1, :] * CAP + rank)
+        slots.append(turn_of[t : t + 1, :] * CAP + rank)
         place = sub == rank
         tok = crow[t : t + 1, :]
         low_sum = low_sum + dot(
@@ -138,35 +160,28 @@
         high_sum = high_sum + dot(
             flags, jnp.where(place, (tok >> 8).astype(F32), 0.0).astype(BF16), 1, 1
         )
-    req[...] = (low_sum + 256.0 * high_sum).astype(I32)
+    asking = (low_sum + 256.0 * high_sum).astype(I32)
+    req[...] = asking.reshape(NX, NY * NC, LANES)
 
     pl.semaphore_wait(barrier, n - 1)
-    asked[0:1, :] = req[0:1, :]
-    for g in range(NY):
-        for a, k in pairs:
-            if (g, a, k) != (0, 0, 0):
-                j = g * group + a * NC + k
-                pltpu.make_async_remote_copy(
-                    src_ref=req.at[pl.ds(j, 1)],
-                    dst_ref=asked.at[pl.ds(j, 1)],
-                    send_sem=req_send,
-                    recv_sem=req_recv.at[g],
-                    device_id={"psg": behind(g, a, k)},
-                    device_id_type=MESH,
-                ).start()
+
+    for a in range(1, NX):
+        where = index(lax.rem(x + NX - a, NX), y, c)
+        push(req.at[a], mid_req.at[a], where, rx_send, rx_recv)
+    mid_req[0] = req[0]
 
     nq = query_ref.shape[0]
+    own_block = qb.at[u, c, pl.ds(pl.multiple_of(v * nq, nq), nq)]
     for a in range(1, NX):
-        px = lax.rem(x + a, NX)
-        pltpu.make_async_remote_copy(
-            src_ref=query_ref,
-            dst_ref=qb.at[y, c, pl.ds(pl.multiple_of(x * nq, nq), nq)],
-            send_sem=qx_send,
-            recv_sem=qx_recv,
-            device_id={"psg": index(px, y, c)},
-            device_id_type=MESH,
-        ).start()
-    qb[y, c, pl.ds(pl.multiple_of(x * nq, nq), nq), :] = query_ref[...]
+        push(query_ref, own_block, at_uv(u, lax.rem(v + a, NX)), qx_send, qx_recv)
+    qb[u, c, pl.ds(pl.multiple_of(v * nq, nq), nq), :] = query_ref[...]
+
+    arrived(mid_req.at[pl.ds(0, NX - 1)], rx_recv)
+    for j in range(1, NY * NC):
+        d, k = j // NC, j % NC
+        where = index(x, lax.rem(y + NY - d, NY), c if k == 0 else other)
+        push(mid_req.at[:, j], asked.at[j], where, ry_send, ry_recv)
+    asked[0] = mid_req[:, 0, :]
 
     slot = jnp.concatenate(slots, axis=0)
     pad = jnp.zeros((LANES - tiles, LANES), F32)
@@ -203,49 +218,41 @@
         goes[:tiles].astype(F32) * goes[1 : tiles + 1].astype(F32), (tiles, LANES)
     )
 
-    up = index(x, lax.rem(y + 1, NY), c)
-    down = index(x, lax.rem(y + NY - 1, NY), c)
+    up = at_uv(lax.rem(u + 1, NY), v)
+    down = at_uv(lax.rem(u + NY - 1, NY), v)
     across = index(x, y, other)
-    n_up, n_down = NY // 2, NY - 1 - NY // 2
+    n_up, n_down = NY - 1 - NY // 2, NY // 2
 
     def pass_on(block, where, send, recv):
-        pltpu.make_async_remote_copy(
-            src_ref=qb.at[block, c],
-            dst_ref=qb.at[block, c],
-            send_sem=send,
-            recv_sem=recv,
-            device_id={"psg": where},
-            device_id_type=MESH,
-        ).start()
-
-    def arrived(ref, sem):
-        pltpu.make_async_copy(ref, ref, sem).wait()
-
-    arrived(qb.at[y, c, pl.ds(0, (NX - 1) * nq)], qx_recv)
-    pass_on(y, up, qup_send, qup_recv.at[0])
-    pass_on(y, down, qdn_send, qdn_recv.at[0])
-    pass_on(y, across, qc_send, qc_recv)
+        push(qb.at[block, c], qb.at[block, c], where, send, recv)
+
+    arrived(qb.at[u, c, pl.ds(0, (NX - 1) * nq)], qx_recv)
+    pass_on(u, up, qup_send, qup_recv.at[0])
+    pass_on(u, down, qdn_send, qdn_recv.at[0])
+    pass_on(u, across, qc_send, qc_recv)
 
     cent_copy.wait()
     half_lane = lax.broadcasted_iota(I32, (CAP, cent.shape[0]), 1).astype(F32)
 
     def ring(s):
-        block = lax.rem(y + NY - s, NY)
-        arrived(qb.at[block, c], qup_recv.at[s - 1])
-        if s < n_up:
-            pass_on(block, up, qup_send, qup_recv.at[s])
+        block = lax.rem(u + s, NY)
+        arrived(qb.at[block, c], qdn_recv.at[s - 1])
+        if s < n_down:
+            pass_on(block, down, qdn_send, qdn_recv.at[s])
         pass_on(block, across, qc_send, qc_recv)
-        if s <= n_down:
-            block = lax.rem(y + s, NY)
-            arrived(qb.at[block, c], qdn_recv.at[s - 1])
-            if s < n_down:
-                pass_on(block, down, qdn_send, qdn_recv.at[s])
+        if s <= n_up:
+            block = lax.rem(u + NY - s, NY)
+            arrived(qb.at[block, c], qup_recv.at[s - 1])
+            if s < n_up:
+                pass_on(block, up, qup_send, qup_recv.at[s])
             pass_on(block, across, qc_send, qc_recv)
 
+    arrived(asked.at[pl.ds(0, NY * NC - 1)], ry_recv)
     for g in range(NY):
-        count = group - 1 if g == 0 else group
-        arrived(asked.at[pl.ds(0, count)], req_recv.at[g])
-        wanted = asked[pl.ds(g * group, group), :].astype(F32).T
+        wanted = jnp.concatenate(
+            [asked[(a + g) % NY * NC + k, a : a + 1, :] for a, k in pairs], axis=0
+        )
+        wanted = wanted.astype(F32).T
         for j in range(group):
             onehot[pl.ds(j * CAP, CAP), :] = (wanted[:CAP, j : j + 1] == half_lane).astype(BF16)
         found = dot(onehot[...], cent[...]).astype(BF16)
@@ -310,7 +317,7 @@
     per = qb.shape[2] // chunk
 
     def maxima(half):
-        @pl.loop(0, NY * NC * per)
+        @pl.loop(0, NY * NC * per, unroll=8)
         def _(i):
             part = qb[
                 i // (NC * per),
@@ -350,24 +357,29 @@
             stack.append(one)
         turned = jnp.concatenate(stack, axis=0).T
         total = jnp.sum(turned.reshape(4, 32, LANES), axis=1)
-        wide[2 * b] = total[0:2]
-        wide[2 * b + 1] = total[2:4]
-
-    for g in range(NY):
-        for a, k in pairs:
-            j = g * group + a * NC + k
-            if j == 0:
-                got[0] = wide[y * 2 + lax.rem(x, 2)]
-                continue
-            px, py, peer = ahead(g, a, k)
-            pltpu.make_async_remote_copy(
-                src_ref=wide.at[py * 2 + lax.rem(px, 2)],
-                dst_ref=got.at[j],
-                send_sem=score_send,
-                recv_sem=score_recv,
-                device_id={"psg": peer},
-                device_id_type=MESH,
-            ).start()
+        wide[b, 0] = total[0:2]
+        wide[b, 1] = total[2:4]
+
+    for d in range(1, NX):
+        py, px = lax.rem(y + d, NY), lax.rem(x + d, NX)
+        push(wide.at[py], mid.at[0, y], index(x, py, c), s1_send, s1_recv)
+        push(wide.at[px], mid.at[1, x], index(px, y, c), s1_send, s1_recv)
+    mid[0, y] = wide[y]
+    mid[1, x] = wide[x]
+    arrived(mid.at[:, pl.ds(0, NX - 1)], s1_recv)
+    for j in range(1, NC * NX):
+        k, d = j // NX, j % NX
+        core = c if k == 0 else other
+        px, py = lax.rem(x + d * (1 - core), NX), lax.rem(y + d * core, NY)
+        parity = lax.rem(px + core * (py - px), 2)
+        push(
+            mid.at[core, :, parity],
+            got.at[pl.ds(j * NY, NY)],
+            index(px, py, core),
+            s2_send,
+            s2_recv,
+        )
+    got[0:NY] = mid[c, :, lax.rem(v, 2)]
 
     cand = cand_ref[...]
     tile = jnp.zeros(cand.shape, I32)
@@ -375,11 +387,14 @@
         table = jnp.broadcast_to(starts[r : r + 1, :], cand.shape)
         value = jnp.take_along_axis(table, cand & (LANES - 1), axis=1)
         tile = jnp.where(cand >> 7 == r, value, tile)
-    source, slot_of = relative(tile // tiles), tile % tiles
+    owner, slot_of = tile // tiles, tile % tiles
+    ox, oy = owner // (NY * NC), (owner // NC) % NY
+    ou, ov = oy + c * (ox - oy), ox + c * (oy - ox)
+    source = (((c - owner) & (NC - 1)) * NX + ((v - ov) & (NX - 1))) * NY + ou
     upper_half = lax.broadcasted_iota(I32, cand.shape, 0) < cand.shape[0] // 2
-    turn = lax.rem(LANES - (c * (NX // 2) + x // 2) * tiles, LANES)
-
-    arrived(got.at[pl.ds(0, n - 1)], score_recv)
+    turn = lax.rem(LANES - (c * (NX // 2) + v // 2) * tiles, LANES)
+
+    arrived(got.at[pl.ds(0, n - NY)], s2_recv)
     tables = [pltpu.roll(got[:, i, :], turn, 1).T for i in range(2)]
     score = jnp.zeros(cand.shape, F32)
     for s in range(tiles):
@@ -388,14 +403,16 @@
         score = jnp.where(slot_of == s, value, score)
     out_ref[...] = score
 
-    arrived(req.at[pl.ds(0, n - 1)], req_send)
+    arrived(req.at[pl.ds(0, NX - 1)], rx_send)
+    arrived(asked.at[pl.ds(0, NY * NC - 1)], ry_send)
     arrived(sent.at[pl.ds(0, (n - 1) * CAP)], row_send)
     arrived(qb.at[0, 0, pl.ds(0, (NX - 1) * nq)], qx_send)
     arrived(qb.at[pl.ds(0, n_up), 0], qup_send)
     arrived(qb.at[pl.ds(0, n_down), 0], qdn_send)
     arrived(qb.at[pl.ds(0, NY), 0], qc_send)
     arrived(head_out, head_send)
-    arrived(got.at[pl.ds(0, n - 1)], score_send)
+    arrived(mid.at[:, pl.ds(0, NX - 1)], s1_send)
+    arrived(got.at[pl.ds(0, n - NY)], s2_send)
 
 
 def per_device(
@@ -426,8 +443,9 @@
         scratch_shapes=[
             pltpu.VMEM(centroids.shape, BF16),
             pltpu.VMEM(residual_codes.shape, I32),
-            pltpu.VMEM((n, LANES), I32),
-            pltpu.VMEM((n, LANES), I32),
+            pltpu.VMEM((NX, NY * NC, LANES), I32),
+            pltpu.VMEM((NX, NY * NC, LANES), I32),
+            pltpu.VMEM((NY * NC, NX, LANES), I32),
             pltpu.VMEM((NX * NC * CAP, centroids.shape[0]), BF16),
             pltpu.VMEM((n * CAP, dim), BF16),
             pltpu.VMEM((n * CAP, dim), BF16),
@@ -440,16 +458,15 @@
             pltpu.VMEM((tiles + 8, n * nq), F32),
             pltpu.VMEM((2, n * nq), F32),
             pltpu.VMEM((2, n * nq), F32),
-            pltpu.VMEM((2 * NY, 2, LANES), F32),
+            pltpu.VMEM((NY, 2, 2, LANES), F32),
+            pltpu.VMEM((NC, NY, 2, 2, LANES), F32),
             pltpu.VMEM((n, 2, LANES), F32),
             pltpu.VMEM((npass, LANES), I32),
             pltpu.VMEM((tiles, LANES), F32),
             pltpu.VMEM((tiles, LANES), F32),
             pltpu.VMEM((tiles, LANES), F32),
             dma((2,)),
-            dma,
-            dma((NY,)),
-            dma,
+            *[dma] * 5,
             dma((NY,)),
             dma,
             dma,
@@ -457,12 +474,7 @@
             dma((NY // 2,)),
             dma,
             dma((NY // 2,)),
-            dma,
-            dma,
-            dma,
-            dma,
-            dma,
-            dma,
+            *[dma] * 8,
         ],
         compiler_params=pltpu.CompilerParams(collective_id=0, has_side_effects=True),
     )(

time: 115 us -> 101 us (0.88)
  Pallas kernels: 112 us -> 98.5 us
    pallas_call x1, Pallas kernels: 112 us -> 98.5 us  [per_device(): pl.pallas_call(kernel, out_shape=jax.ShapeDtypeStruct((ncand, LANES), F32...]
where the time goes in v1:
time: 101 us
  Pallas kernels  98.5 us (98%)
  local copies, waits for them, and re-layouts  2.56 us (3%)
    pallas_call x1, Pallas kernels, per_device(): pl.pallas_call(kernel, out_shape=jax.ShapeDtypeStruct((ncand, LANES), F32...  98.5 us

profile of v1, /device:TPU:513, one launch (start us, length us, event | category | flops | bytes accessed | tf_op | source)
XLA Modules:
  0.0 101.0 jit_solution(16447152275590795108)
XLA Ops:
  0.0 0.0 copy-start
  0.0 0.7 copy-done
  0.7 0.6 reshape.26.cand_ref
  1.3 98.5 %shard_map.91 = f32[8,128]{1,0:T(8,128)} custom-call(s32[16,128]{1,0:T(8,128)} %bitcast.6, s32[16,128]{1,0:T(8,128)} %bitcast.7, bf16[512,128]{1,0:T(8,128)(2,1)} %cent_hbm.1, s32[2048,128]{1,0:T(8,128)} %code_hbm.1, f32[4,128]{1,0:T(4,128)} %bw_ref.1, s32[10,128]{1,0:T(8,128)} %bitcast.8, s32[10,128]{1,0:T(8,128)} %bitcast.9, bf16[64,128]{1,0:T(8,128)(2,1)} %bitcast.5, ...), custom_call_target="tpu_custom_call" | custom-call | tf_op jit(solution)/shard_map/pallas_call | solution.py:438
  99.8 1.3 %reshape.27 = f32[2,512]{1,0:T(2,128)} reshape(f32[8,128]{1,0:T(8,128)} %shard_map.91) | data formatting | bytes 8192 | tf_op jit(solution)/shard_map/reshape | solution.py:491
Async XLA Ops:
  0.0 0.7 copy-start

commit v2 on v1

--- a/solution.py
+++ b/solution.py
@@ -49,7 +49,6 @@
     head_out,
     head_in,
     wide,
-    mid,
     got,
     starts,
     fills,
@@ -72,10 +71,8 @@
     qc_recv,
     head_send,
     head_recv,
-    s1_send,
-    s1_recv,
-    s2_send,
-    s2_recv,
+    score_send,
+    score_recv,
 ):
     n = NX * NY * NC
     tiles = owner_ref.shape[0]
@@ -118,6 +115,10 @@
     u, v = y + c * (x - y), x + c * (y - x)
 
     pairs = [(a, k) for a in range(NX) for k in range(NC)]
+    far = sorted(
+        [(g, a, k) for g in range(NY) for a, k in pairs if (g, a, k) != (0, 0, 0)],
+        key=lambda p: -min(p[1], NX - p[1]) - min((p[0] + p[1]) % NY, -(p[0] + p[1]) % NY),
+    )
     group = NX * NC
     gslots = group * CAP
 
@@ -183,6 +184,63 @@
         push(mid_req.at[:, j], asked.at[j], where, ry_send, ry_recv)
     asked[0] = mid_req[:, 0, :]
 
+    up = at_uv(lax.rem(u + 1, NY), v)
+    down = at_uv(lax.rem(u + NY - 1, NY), v)
+    across = index(x, y, other)
+    n_up, n_down = NY - 1 - NY // 2, NY // 2
+
+    def pass_on(block, where, send, recv):
+        push(qb.at[block, c], qb.at[block, c], where, send, recv)
+
+    arrived(qb.at[u, c, pl.ds(0, (NX - 1) * nq)], qx_recv)
+    pass_on(u, up, qup_send, qup_recv.at[0])
+    pass_on(u, down, qdn_send, qdn_recv.at[0])
+    pass_on(u, across, qc_send, qc_recv)
+
+    cent_copy.wait()
+    half_lane = lax.broadcasted_iota(I32, (CAP, cent.shape[0]), 1).astype(F32)
+
+    def ring(s):
+        block = lax.rem(u + s, NY)
+        arrived(qb.at[block, c], qdn_recv.at[s - 1])
+        if s < n_down:
+            pass_on(block, down, qdn_send, qdn_recv.at[s])
+        pass_on(block, across, qc_send, qc_recv)
+        if s <= n_up:
+            block = lax.rem(u + NY - s, NY)
+            arrived(qb.at[block, c], qup_recv.at[s - 1])
+            if s < n_up:
+                pass_on(block, up, qup_send, qup_recv.at[s])
+            pass_on(block, across, qc_send, qc_recv)
+
+    ring(1)
+    arrived(asked.at[pl.ds(0, NY * NC - 1)], ry_recv)
+    for g in range(NY):
+        wanted = jnp.concatenate(
+            [asked[(a + g) % NY * NC + k, a : a + 1, :] for a, k in pairs], axis=0
+        )
+        wanted = wanted.astype(F32).T
+        for j in range(group):
+            onehot[pl.ds(j * CAP, CAP), :] = (wanted[:CAP, j : j + 1] == half_lane).astype(BF16)
+        found = dot(onehot[...], cent[...]).astype(BF16)
+        sent[pl.ds(g * gslots, gslots), :] = found
+        if g == 0:
+            fetched[pl.ds(0, CAP), :] = found[:CAP]
+        for a, k in pairs:
+            if (g, a, k) != (0, 0, 0):
+                at = pl.ds((g * group + a * NC + k) * CAP, CAP)
+                pltpu.make_async_remote_copy(
+                    src_ref=sent.at[at],
+                    dst_ref=fetched.at[at],
+                    send_sem=row_send,
+                    recv_sem=row_recv.at[g],
+                    device_id={"psg": ahead(g, a, k)[2]},
+                    device_id_type=MESH,
+                ).start()
+        if g == 3:
+            ring(2)
+
+    ring(3)
     slot = jnp.concatenate(slots, axis=0)
     pad = jnp.zeros((LANES - tiles, LANES), F32)
     low_t = jnp.concatenate([(slot & 255).astype(F32), pad], axis=0).T
@@ -218,70 +276,23 @@
         goes[:tiles].astype(F32) * goes[1 : tiles + 1].astype(F32), (tiles, LANES)
     )
 
-    up = at_uv(lax.rem(u + 1, NY), v)
-    down = at_uv(lax.rem(u + NY - 1, NY), v)
-    across = index(x, y, other)
-    n_up, n_down = NY - 1 - NY // 2, NY // 2
-
-    def pass_on(block, where, send, recv):
-        push(qb.at[block, c], qb.at[block, c], where, send, recv)
-
-    arrived(qb.at[u, c, pl.ds(0, (NX - 1) * nq)], qx_recv)
-    pass_on(u, up, qup_send, qup_recv.at[0])
-    pass_on(u, down, qdn_send, qdn_recv.at[0])
-    pass_on(u, across, qc_send, qc_recv)
-
-    cent_copy.wait()
-    half_lane = lax.broadcasted_iota(I32, (CAP, cent.shape[0]), 1).astype(F32)
-
-    def ring(s):
-        block = lax.rem(u + s, NY)
-        arrived(qb.at[block, c], qdn_recv.at[s - 1])
-        if s < n_down:
-            pass_on(block, down, qdn_send, qdn_recv.at[s])
-        pass_on(block, across, qc_send, qc_recv)
-        if s <= n_up:
-            block = lax.rem(u + NY - s, NY)
-            arrived(qb.at[block, c], qup_recv.at[s - 1])
-            if s < n_up:
-                pass_on(block, up, qup_send, qup_recv.at[s])
-            pass_on(block, across, qc_send, qc_recv)
-
-    arrived(asked.at[pl.ds(0, NY * NC - 1)], ry_recv)
-    for g in range(NY):
-        wanted = jnp.concatenate(
-            [asked[(a + g) % NY * NC + k, a : a + 1, :] for a, k in pairs], axis=0
-        )
-        wanted = wanted.astype(F32).T
-        for j in range(group):
-            onehot[pl.ds(j * CAP, CAP), :] = (wanted[:CAP, j : j + 1] == half_lane).astype(BF16)
-        found = dot(onehot[...], cent[...]).astype(BF16)
-        sent[pl.ds(g * gslots, gslots), :] = found
-        if g == 0:
-            fetched[pl.ds(0, CAP), :] = found[:CAP]
-        for a, k in pairs:
-            if (g, a, k) != (0, 0, 0):
-                at = pl.ds((g * group + a * NC + k) * CAP, CAP)
-                pltpu.make_async_remote_copy(
-                    src_ref=sent.at[at],
-                    dst_ref=fetched.at[at],
-                    send_sem=row_send,
-                    recv_sem=row_recv.at[g],
-                    device_id={"psg": ahead(g, a, k)[2]},
-                    device_id_type=MESH,
-                ).start()
-        if g % 2 == 0:
-            ring(g // 2 + 1)
-
     code_copy.wait()
 
-    @pl.loop(0, tiles)
+    @pl.loop(0, tiles, unroll=4)
     def _(t):
         at = pl.ds(pl.multiple_of(t * TILE, TILE), TILE)
         v = code[at, :]
         first = jnp.where(v == 0, bw_ref[0:1, :], bw_ref[1:2, :])
         second = jnp.where(v == 2, bw_ref[2:3, :], bw_ref[3:4, :])
         res[at, :] = jnp.where(v < 2, first, second)
+
+    cand = cand_ref[...]
+    tile = jnp.zeros(cand.shape, I32)
+    for r in range(npass):
+        table = jnp.broadcast_to(starts[r : r + 1, :], cand.shape)
+        value = jnp.take_along_axis(table, cand & (LANES - 1), axis=1)
+        tile = jnp.where(cand >> 7 == r, value, tile)
+    ring(4)
 
     span = 4 * TILE
     for g in range(NY):
@@ -292,7 +303,7 @@
             [fetched[pl.ds(base, 256), :], fetched[pl.ds(base + 256, 256), :]], axis=1
         )
 
-        @pl.loop(0, tiles * TILE // span)
+        @pl.loop(0, tiles * TILE // span, unroll=4)
         def _(i):
             at = pl.ds(pl.multiple_of(i * span, span), span)
             picked = dot(low[at, :], both)
@@ -301,7 +312,7 @@
             keep = jnp.where(which == float(2 * g + 1), picked[:, LANES:], keep)
             acc[at, :] = jnp.where(which == float(2 * g), picked[:, :LANES], keep)
 
-    @pl.loop(0, tiles)
+    @pl.loop(0, tiles, unroll=8)
     def _(t):
         at = pl.ds(pl.multiple_of(t * TILE, TILE), TILE)
         summed = acc[at, :] + res[at, :]
@@ -360,41 +371,26 @@
         wide[b, 0] = total[0:2]
         wide[b, 1] = total[2:4]
 
-    for d in range(1, NX):
-        py, px = lax.rem(y + d, NY), lax.rem(x + d, NX)
-        push(wide.at[py], mid.at[0, y], index(x, py, c), s1_send, s1_recv)
-        push(wide.at[px], mid.at[1, x], index(px, y, c), s1_send, s1_recv)
-    mid[0, y] = wide[y]
-    mid[1, x] = wide[x]
-    arrived(mid.at[:, pl.ds(0, NX - 1)], s1_recv)
-    for j in range(1, NC * NX):
-        k, d = j // NX, j % NX
-        core = c if k == 0 else other
-        px, py = lax.rem(x + d * (1 - core), NX), lax.rem(y + d * core, NY)
-        parity = lax.rem(px + core * (py - px), 2)
+    for g, a, k in far:
+        px, py, peer = ahead(g, a, k)
+        pc = c if k == 0 else other
+        pu, pv = py + pc * (px - py), px + pc * (py - px)
         push(
-            mid.at[core, :, parity],
-            got.at[pl.ds(j * NY, NY)],
-            index(px, py, core),
-            s2_send,
-            s2_recv,
+            wide.at[pu, lax.rem(pv, 2)],
+            got.at[g * group + a * NC + k],
+            peer,
+            score_send,
+            score_recv,
         )
-    got[0:NY] = mid[c, :, lax.rem(v, 2)]
-
-    cand = cand_ref[...]
-    tile = jnp.zeros(cand.shape, I32)
-    for r in range(npass):
-        table = jnp.broadcast_to(starts[r : r + 1, :], cand.shape)
-        value = jnp.take_along_axis(table, cand & (LANES - 1), axis=1)
-        tile = jnp.where(cand >> 7 == r, value, tile)
+    got[0] = wide[u, lax.rem(v, 2)]
+
     owner, slot_of = tile // tiles, tile % tiles
-    ox, oy = owner // (NY * NC), (owner // NC) % NY
-    ou, ov = oy + c * (ox - oy), ox + c * (oy - ox)
-    source = (((c - owner) & (NC - 1)) * NX + ((v - ov) & (NX - 1))) * NY + ou
+    dx, dy, dc = shift(owner)
+    source = ((dy - dx) & (NY - 1)) * (NX * NC) + dx * NC + dc
     upper_half = lax.broadcasted_iota(I32, cand.shape, 0) < cand.shape[0] // 2
     turn = lax.rem(LANES - (c * (NX // 2) + v // 2) * tiles, LANES)
 
-    arrived(got.at[pl.ds(0, n - NY)], s2_recv)
+    arrived(got.at[pl.ds(0, n - 1)], score_recv)
     tables = [pltpu.roll(got[:, i, :], turn, 1).T for i in range(2)]
     score = jnp.zeros(cand.shape, F32)
     for s in range(tiles):
@@ -411,8 +407,7 @@
     arrived(qb.at[pl.ds(0, n_down), 0], qdn_send)
     arrived(qb.at[pl.ds(0, NY), 0], qc_send)
     arrived(head_out, head_send)
-    arrived(mid.at[:, pl.ds(0, NX - 1)], s1_send)
-    arrived(got.at[pl.ds(0, n - NY)], s2_send)
+    arrived(got.at[pl.ds(0, n - 1)], score_send)
 
 
 def per_device(
@@ -459,7 +454,6 @@
             pltpu.VMEM((2, n * nq), F32),
             pltpu.VMEM((2, n * nq), F32),
             pltpu.VMEM((NY, 2, 2, LANES), F32),
-            pltpu.VMEM((NC, NY, 2, 2, LANES), F32),
             pltpu.VMEM((n, 2, LANES), F32),
             pltpu.VMEM((npass, LANES), I32),
             pltpu.VMEM((tiles, LANES), F32),
@@ -474,7 +468,7 @@
             dma((NY // 2,)),
             dma,
             dma((NY // 2,)),
-            *[dma] * 8,
+            *[dma] * 6,
         ],
         compiler_params=pltpu.CompilerParams(collective_id=0, has_side_effects=True),
     )(

time: 101 us -> 95.4 us (0.945)
  Pallas kernels: 98.5 us -> 92.7 us
    pallas_call x1, Pallas kernels: 98.5 us -> 92.7 us  [per_device(): pl.pallas_call(kernel, out_shape=jax.ShapeDtypeStruct((ncand, LANES), F32...]
where the time goes in v2:
time: 95.4 us; the launch traced here: 95.2 us
  Pallas kernels  92.7 us (97%)
  local copies, waits for them, and re-layouts  2.56 us (3%)
    pallas_call x1, Pallas kernels, per_device(): pl.pallas_call(kernel, out_shape=jax.ShapeDtypeStruct((ncand, LANES), F32...  92.7 us

profile of v2, /device:TPU:513, one launch (start us, length us, event | category | flops | bytes accessed | tf_op | source)
XLA Modules:
  0.0 95.2 jit_solution(7871892298216836946)
XLA Ops:
  0.0 0.0 copy-start
  0.0 0.7 copy-done
  0.7 0.6 reshape.26.cand_ref
  1.3 92.7 %shard_map.91 = f32[8,128]{1,0:T(8,128)} custom-call(s32[16,128]{1,0:T(8,128)} %bitcast.6, s32[16,128]{1,0:T(8,128)} %bitcast.7, bf16[512,128]{1,0:T(8,128)(2,1)} %cent_hbm.1, s32[2048,128]{1,0:T(8,128)} %code_hbm.1, f32[4,128]{1,0:T(4,128)} %bw_ref.1, s32[10,128]{1,0:T(8,128)} %bitcast.8, s32[10,128]{1,0:T(8,128)} %bitcast.9, bf16[64,128]{1,0:T(8,128)(2,1)} %bitcast.5, ...), custom_call_target="tpu_custom_call" | custom-call | tf_op jit(solution)/shard_map/pallas_call | solution.py:433
  94.0 1.3 %reshape.27 = f32[2,512]{1,0:T(2,128)} reshape(f32[8,128]{1,0:T(8,128)} %shard_map.91) | data formatting | bytes 8192 | tf_op jit(solution)/shard_map/reshape | solution.py:485
Async XLA Ops:
  0.0 0.7 copy-start

commit v3 on v2

--- a/solution.py
+++ b/solution.py
@@ -123,12 +123,15 @@
     gslots = group * CAP
 
     barrier = pltpu.get_barrier_semaphore()
-    for g in range(NY):
-        for a, k in pairs:
-            if (g, a, k) != (0, 0, 0):
-                pl.semaphore_signal(
-                    barrier, inc=1, device_id={"psg": ahead(g, a, k)[2]}, device_id_type=MESH
-                )
+    greeted = [index(lax.rem(x + d, NX), y, c) for d in range(1, NX)]
+    greeted += [
+        index(x, lax.rem(y + d, NY), c if k == 0 else other)
+        for d in range(NY)
+        for k in range(NC)
+        if (d, k) != (0, 0)
+    ]
+    for peer in greeted:
+        pl.semaphore_signal(barrier, inc=1, device_id={"psg": peer}, device_id_type=MESH)
     cent_copy = pltpu.make_async_copy(cent_hbm, cent, load_sem.at[0])
     cent_copy.start()
     code_copy = pltpu.make_async_copy(code_hbm, code, load_sem.at[1])
@@ -142,29 +145,30 @@
     rel = (dx * NY + dy) * NC + dc
     turn_of = ((dy - dx) & (NY - 1)) * (NX * NC) + dx * NC + dc
     crow = row_ref[...]
+    members = [sub == rel[t : t + 1, :] for t in range(tiles)]
+    flags = [m.astype(BF16) for m in members]
+    running = dot(jnp.concatenate(flags, axis=0), jnp.concatenate([upper, ones], axis=1))
     carry = jnp.zeros((LANES, LANES), F32)
-    low_sum = jnp.zeros((LANES, LANES), F32)
-    high_sum = jnp.zeros((LANES, LANES), F32)
-    slots = []
+    slots, lows, highs = [], [], []
     for t in range(tiles):
-        member = sub == rel[t : t + 1, :]
-        flags = member.astype(BF16)
-        running = dot(flags, upper) + carry
-        carry = carry + dot(flags, ones)
-        rank = jnp.sum(jnp.where(member, running, 0.0), axis=0, keepdims=True).astype(I32) - 1
+        part = running[t * LANES : (t + 1) * LANES, :]
+        count = jnp.where(members[t], part[:, :LANES] + carry, 0.0)
+        carry = carry + part[:, LANES:]
+        rank = jnp.sum(count, axis=0, keepdims=True).astype(I32) - 1
         slots.append(turn_of[t : t + 1, :] * CAP + rank)
         place = sub == rank
         tok = crow[t : t + 1, :]
-        low_sum = low_sum + dot(
-            flags, jnp.where(place, (tok & 255).astype(F32), 0.0).astype(BF16), 1, 1
-        )
-        high_sum = high_sum + dot(
-            flags, jnp.where(place, (tok >> 8).astype(F32), 0.0).astype(BF16), 1, 1
-        )
+        lows.append(jnp.where(place, (tok & 255).astype(F32), 0.0).astype(BF16))
+        highs.append(jnp.where(place, (tok >> 8).astype(F32), 0.0).astype(BF16))
+    values = jnp.concatenate(
+        [jnp.concatenate(lows, axis=1), jnp.concatenate(highs, axis=1)], axis=0
+    )
+    summed = dot(jnp.concatenate(flags, axis=1), values, 1, 1)
+    low_sum, high_sum = summed[:, :LANES], summed[:, LANES:]
     asking = (low_sum + 256.0 * high_sum).astype(I32)
     req[...] = asking.reshape(NX, NY * NC, LANES)
 
-    pl.semaphore_wait(barrier, n - 1)
+    pl.semaphore_wait(barrier, len(greeted))
 
     for a in range(1, NX):
         where = index(lax.rem(x + NX - a, NX), y, c)
@@ -328,7 +332,7 @@
     per = qb.shape[2] // chunk
 
     def maxima(half):
-        @pl.loop(0, NY * NC * per, unroll=8)
+        @pl.loop(0, NY * NC * per, unroll=16)
         def _(i):
             part = qb[
                 i // (NC * per),

time: 95.4 us -> 91.3 us (0.957)
  Pallas kernels: 92.7 us -> 88.5 us
    pallas_call x1, Pallas kernels: 92.7 us -> 88.5 us  [per_device(): pl.pallas_call(kernel, out_shape=jax.ShapeDtypeStruct((ncand, LANES), F32...]
where the time goes in v3:
time: 91.3 us; the launch traced here: 91 us
  Pallas kernels  88.5 us (97%)
  local copies, waits for them, and re-layouts  2.56 us (3%)
    pallas_call x1, Pallas kernels, per_device(): pl.pallas_call(kernel, out_shape=jax.ShapeDtypeStruct((ncand, LANES), F32...  88.5 us

profile of v3, /device:TPU:513, one launch (start us, length us, event | category | flops | bytes accessed | tf_op | source)
XLA Modules:
  0.0 91.0 jit_solution(547334293175587222)
XLA Ops:
  0.0 0.0 copy-start
  0.0 0.7 copy-done
  0.7 0.6 reshape.26.cand_ref
  1.3 88.5 %shard_map.91 = f32[8,128]{1,0:T(8,128)} custom-call(s32[16,128]{1,0:T(8,128)} %bitcast.6, s32[16,128]{1,0:T(8,128)} %bitcast.7, bf16[512,128]{1,0:T(8,128)(2,1)} %cent_hbm.1, s32[2048,128]{1,0:T(8,128)} %code_hbm.1, f32[4,128]{1,0:T(4,128)} %bw_ref.1, s32[10,128]{1,0:T(8,128)} %bitcast.8, s32[10,128]{1,0:T(8,128)} %bitcast.9, bf16[64,128]{1,0:T(8,128)(2,1)} %bitcast.5, ...), custom_call_target="tpu_custom_call" | custom-call | tf_op jit(solution)/shard_map/pallas_call | solution.py:437
  89.8 1.3 %reshape.27 = f32[2,512]{1,0:T(2,128)} reshape(f32[8,128]{1,0:T(8,128)} %shard_map.91) | data formatting | bytes 8192 | tf_op jit(solution)/shard_map/reshape | solution.py:489
Async XLA Ops:
  0.0 0.7 copy-start

commit v4 on v3

--- a/solution.py
+++ b/solution.py
@@ -290,7 +290,12 @@
         second = jnp.where(v == 2, bw_ref[2:3, :], bw_ref[3:4, :])
         res[at, :] = jnp.where(v < 2, first, second)
 
-    cand = cand_ref[...]
+    cuts = [
+        (i, slice(j, j + LANES))
+        for i in range(cand_ref.shape[0])
+        for j in range(0, cand_ref.shape[1], LANES)
+    ]
+    cand = jnp.concatenate([cand_ref[i : i + 1, at] for i, at in cuts], axis=0)
     tile = jnp.zeros(cand.shape, I32)
     for r in range(npass):
         table = jnp.broadcast_to(starts[r : r + 1, :], cand.shape)
@@ -401,7 +406,8 @@
         table = jnp.where(upper_half, tables[0][s : s + 1, :], tables[1][s : s + 1, :])
         value = jnp.take_along_axis(table, source, axis=1)
         score = jnp.where(slot_of == s, value, score)
-    out_ref[...] = score
+    for r, (i, at) in enumerate(cuts):
+        out_ref[i : i + 1, at] = score[r : r + 1, :]
 
     arrived(req.at[pl.ds(0, NX - 1)], rx_send)
     arrived(asked.at[pl.ds(0, NY * NC - 1)], ry_send)
@@ -429,14 +435,13 @@
     tok, dim = residual_codes.shape
     tiles = tok // TILE
     nq = queries.shape[0] * queries.shape[1]
-    ncand = candidates.size // LANES
     npass = tile_count.shape[0] // LANES
     dma = pltpu.SemaphoreType.DMA
     vmem = pl.BlockSpec(memory_space=pltpu.VMEM)
     anywhere = pl.BlockSpec(memory_space=pl.ANY)
-    score = pl.pallas_call(
+    return pl.pallas_call(
         kernel,
-        out_shape=jax.ShapeDtypeStruct((ncand, LANES), F32),
+        out_shape=jax.ShapeDtypeStruct(candidates.shape, F32),
         in_specs=[vmem, vmem, anywhere, anywhere, vmem, vmem, vmem, vmem, vmem],
         out_specs=vmem,
         scratch_shapes=[
@@ -484,9 +489,8 @@
         tile_count.reshape(npass, LANES),
         last_fill.reshape(npass, LANES),
         queries.reshape(nq, dim),
-        candidates.reshape(ncand, LANES),
+        candidates,
     )
-    return score.reshape(candidates.shape)
 
 
 def solution(mesh):

time: 91.3 us -> 89.9 us (0.985)
  local copies, waits for them, and re-layouts: 2.56 us -> 1.28 us
    reshape x2 -> x0, local copies, waits for them, and re-layouts: 1.87 us -> none  [the longest x1 1.27 us: per_device(): return score.reshape(candidates.shape)]
where the time goes in v4:
time: 89.9 us; the launch traced here: 89.8 us
  Pallas kernels  88.5 us (98%)
  local copies, waits for them, and re-layouts  1.28 us (1%)
    pallas_call x1, Pallas kernels, per_device(): pl.pallas_call(kernel, out_shape=jax.ShapeDtypeStruct(candidates.shape, F...  88.5 us

profile of v4, /device:TPU:513, one launch (start us, length us, event | category | flops | bytes accessed | tf_op | source)
XLA Modules:
  0.0 89.8 jit_solution(16939685394032186742)
XLA Ops:
  0.0 88.5 %shard_map.91 = f32[2,512]{1,0:T(2,128)} custom-call(s32[16,128]{1,0:T(8,128)} %bitcast.6, s32[16,128]{1,0:T(8,128)} %bitcast.7, bf16[512,128]{1,0:T(8,128)(2,1)} %cent_hbm.1, s32[2048,128]{1,0:T(8,128)} %code_hbm.1, f32[4,128]{1,0:T(4,128)} %bw_ref.1, s32[10,128]{1,0:T(8,128)} %bitcast.8, s32[10,128]{1,0:T(8,128)} %bitcast.9, bf16[64,128]{1,0:T(8,128)(2,1)} %bitcast.5, ...), custom_call_target="tpu_custom_call" | custom-call | tf_op jit(solution)/shard_map/pallas_call | solution.py:442
  88.5 1.3 %copy.11 = f32[2,512]{1,0:T(2,128)} copy(f32[2,512]{1,0:T(2,128)} %shard_map.91) | data formatting | bytes 8192
